TPU v7x, 512 devices: a whole 4x4x16 slice. The times are simulated.
512 devices in a mesh: aux: 16 (over z_lo, y), row: 32 (over x, z_hi, core).
Axes of the slice: x: 4, y: 4, z: 16 (z_hi: 4, z_lo: 4; z = z_hi * 4 + z_lo), core: 2. Of those that a mesh axis runs over, the one named last changes fastest.
Arguments:
- coeff: bfloat16 [800, 4096], P(None, 'row'), may hold values from -0.109375 to 0.109375
- band: bfloat16 [32, 384, 4096], P('aux', None, 'row'), may hold values from -6 to 6
- pairs: int32 [32, 32], replicated, may hold values from 0 to 1, as said below
Outputs:
- exchange_k: float32 [4096, 4096], P('row', 'aux')
Inputs may be any that keep to these rules, and one draw needn't show every extreme that they name: pairs is symmetric, holds only 0 and 1, and its diagonal is 1; how many blocks a row keeps differs from row to row.
All inputs are finite; a program needn't handle non-finite values.
Results may differ from a plain program's by a relative error of at most 0.0012.
Values may be sent and summed in bfloat16 or wider, within the bound.
No kernel may reach another device: no remote copies, remote signals or barrier semaphores. Data moves between devices by JAX's collectives and lax.ppermute only.
A program may use at most 64 MiB of HBM per device.

v0:
```python
import jax
import jax.numpy as jnp
from jax import lax
from jax.sharding import Mesh
from jax.sharding import PartitionSpec as P

ROW = ("row_0", "row_1", "row_2")


def padded_2(cells, sides, width):
    for axis, dim in sides:
        count = lax.axis_size(axis)
        ends = count - 1
        head = lax.slice_in_dim(cells, 0, width, axis=dim)
        tail = lax.slice_in_dim(cells, cells.shape[dim] - width, cells.shape[dim], axis=dim)
        cells = jnp.concatenate(
            [
                lax.ppermute(tail, axis, [(i, (i + 1) % count) for i in range(ends)]),
                cells,
                lax.ppermute(head, axis, [((i + 1) % count, i) for i in range(ends)]),
            ],
            axis=dim,
        )
    return cells


def laid_out(blocks, dim):
    lengths = list(blocks.shape[1:])
    lengths[dim] *= blocks.shape[0]
    return jnp.moveaxis(blocks, 0, dim).reshape(lengths)


def gather_in_order(shard, axes, turns):
    blocks = shard[None]
    for k in turns:
        blocks = lax.all_gather(blocks, axes[k], axis=0, tiled=True)
    held = [lax.axis_size(axes[k]) for k in reversed(turns)]
    blocks = blocks.reshape(*held, *shard.shape)
    turned = sorted(range(len(turns)), key=lambda place: turns[len(turns) - 1 - place])
    return blocks.transpose(*turned, *range(len(turns), blocks.ndim)).reshape(-1, *shard.shape)


def whole_of(shard, axes, turns, dim):
    return laid_out(gather_in_order(shard, axes, turns), dim)


def in_blocks(shard, dim, devices):
    before, after = (shard.shape[:dim], shard.shape[dim + 1 :])
    return jnp.moveaxis(shard.reshape(*before, devices, -1, *after), dim, 0)


def sum_at_owner(shard, axis, dim):
    blocks = in_blocks(shard, dim, lax.axis_size(axis))
    arrived = lax.all_to_all(blocks, axis, split_axis=0, concat_axis=0, tiled=True)
    return arrived.sum(axis=0)


def on_device(coeff, band, pairs):
    block = band.shape[2]
    row_count = lax.axis_size(ROW)
    own_index = lax.axis_index(ROW)
    padded = padded_2(coeff, ((ROW, 1),), block)
    half_factor = jnp.einsum(
        "ij,qjm->qim", padded, band, preferred_element_type=jnp.float32
    ).astype(jnp.bfloat16)
    stacked = half_factor.reshape(-1, block)
    own_row = lax.dynamic_index_in_dim(pairs, own_index, 0, keepdims=False)
    piece = whole_of(stacked, ROW, (1, 0, 2), 1)
    product = lax.dot_general(
        stacked, piece, (((0,), (0,)), ((), ())), preferred_element_type=jnp.float32
    )
    column_block = jnp.arange(piece.shape[1], dtype=jnp.int32) // block
    onehot = (column_block[:, None] == jnp.arange(row_count, dtype=jnp.int32)[None, :]).astype(
        jnp.float32
    )
    screen = jnp.dot(onehot, own_row.astype(jnp.float32))
    k_rows = product * screen[None, :]
    return sum_at_owner(k_rows, "aux", 1)


def solution(mesh):
    torus = Mesh(
        mesh.devices.reshape(mesh.shape["aux"], 4, 4, 2), ("aux", "row_0", "row_1", "row_2")
    )
    in_specs = (P(None, ROW), P("aux", None, ROW), P())
    out_specs = P(ROW, "aux")
    return jax.shard_map(
        on_device, mesh=torus, in_specs=in_specs, out_specs=out_specs, check_vma=False
    )
```

profile of v0, /device:TPU:2, one launch (start us, length us, event | category | flops | bytes accessed | tf_op | source)
XLA Modules:
  0.0 297.3 jit_solution(3850492844797709839)
XLA Ops:
  6.5 0.0 copy-start
  6.5 0.0 all-gather.4.cloned.1.call-start
  6.5 12.3 %collective-permute-start.1 = (bf16[800,128]{1,0:T(8,128)(2,1)}, bf16[800,128]{1,0:T(8,128)(2,1)S(1)}, u32[]{:S(2)}, u32[]{:S(2)}) collective-permute-start(bf16[800,128]{1,0:T(8,128)(2,1)} %param.3), channel_id=1, source_target_pairs={{1,0},{2,1},{3,2},{4,3},{5,4},{6,5},{7,6},{8,7},{9,8},{10,9},{11,1... | collective-permute-start | bytes 614408 | tf_op jit(solution)/shard_map/ppermute | solution.py:20
  18.8 1.9 collective-permute-start
  20.7 8.3 %collective-permute-done.1 = bf16[800,128]{1,0:T(8,128)(2,1)S(1)} collective-permute-done((bf16[800,128]{1,0:T(8,128)(2,1)}, bf16[800,128]{1,0:T(8,128)(2,1)S(1)}, u32[]{:S(2)}, u32[]{:S(2)}) %collective-permute-start.1) | collective-permute-done | bytes 204832 | tf_op jit(solution)/shard_map/ppermute | solution.py:20
  29.0 8.6 %collective-permute-done = bf16[800,128]{1,0:T(8,128)(2,1)S(1)} collective-permute-done((bf16[800,128]{1,0:T(8,128)(2,1)}, bf16[800,128]{1,0:T(8,128)(2,1)S(1)}, u32[]{:S(2)}, u32[]{:S(2)}) %collective-permute-start) | collective-permute-done | bytes 204832 | tf_op jit(solution)/shard_map/ppermute | solution.py:18
  37.6 0.0 copy-done
  37.6 2.1 convolution_convert_fusion
  39.7 0.0 all-gather.4.cloned.1.call-update
  39.7 0.0 all-gather.6.cloned.1.call-start
  39.8 72.0 %all-gather.4.cloned.1.call-done = bf16[4,1600,128]{2,1,0:T(8,128)(2,1)} async-done(((bf16[1,1600,128]{2,1,0:T(8,128)(2,1)}), bf16[4,1600,128]{2,1,0:T(8,128)(2,1)}) %all-gather.4.cloned.1.call-update) | async-done | bytes 1638416 | tf_op jit(solution)/shard_map/all_gather | solution.py:36
  111.8 0.0 all-gather.6.cloned.1.call-update
  111.8 0.0 all-gather.8.cloned.1.call-start
  111.9 73.6 %all-gather.6.cloned.1.call-done = bf16[16,1600,128]{2,1,0:T(8,128)(2,1)} async-done(((bf16[4,1600,128]{2,1,0:T(8,128)(2,1)}), bf16[16,1600,128]{2,1,0:T(8,128)(2,1)}) %all-gather.6.cloned.1.call-update) | async-done | bytes 6553616 | tf_op jit(solution)/shard_map/all_gather | solution.py:36
  185.5 0.0 all-gather.8.cloned.1.call-update
  185.5 0.9 fusion.10
  186.4 38.0 %all-gather.8.cloned.1.call-done = bf16[32,1600,128]{2,1,0:T(8,128)(2,1)} async-done(((bf16[16,1600,128]{2,1,0:T(8,128)(2,1)}), bf16[32,1600,128]{2,1,0:T(8,128)(2,1)}) %all-gather.8.cloned.1.call-update) | async-done | bytes 13107216 | tf_op jit(solution)/shard_map/all_gather | solution.py:36
  224.4 0.0 copy-start.1
  224.4 6.6 %copy.10 = bf16[4,4,2,1600,128]{4,3,2,1,0:T(8,128)(2,1)S(1)} copy(bf16[4,4,2,1600,128]{4,3,1,0,2:T(8,128)(2,1)} %bitcast.34) | data formatting | bytes 26214400 | tf_op jit(solution)/shard_map/transpose | solution.py:40
  231.0 0.0 copy-done.1
  231.0 2.1 fusion.3
  233.1 0.2 copy.22
  233.3 56.7 %all_to_all.5 = f32[16,128,256]{2,1,0:T(8,128)S(1)} all-to-all(f32[16,128,256]{2,1,0:T(8,128)S(1)} %bitcast.36), channel_id=1, replica_groups=mesh['aux'=16,'row_0'=4,'row_1'=4,'row_2'=2] {'aux'}, dimensions={0} | all-to-all | bytes 4194304 | tf_op jit(solution)/shard_map/all_to_all | solution.py:54
  290.0 0.8 reduce_sum.9
  (1 shorter events, 0.0 us)
Async XLA Ops:
  6.5 31.1 %copy-start = (bf16[2,384,128]{2,1,0:T(8,128)(2,1)S(1)}, bf16[2,384,128]{2,1,0:T(8,128)(2,1)}, u32[]{:S(2)}) copy-start(bf16[2,384,128]{2,1,0:T(8,128)(2,1)} %param.4) | copy-start | bytes 589828
  6.5 105.2 %all-gather.4.cloned.1.call-start = ((), (), s32[]{:S(2)}) async-start(), calls=%async_computation.1 | async-start | bytes 2048000 | tf_op jit(solution)/shard_map/all_gather | solution.py:36
  6.5 22.5 %collective-permute-start.1 = (bf16[800,128]{1,0:T(8,128)(2,1)}, bf16[800,128]{1,0:T(8,128)(2,1)S(1)}, u32[]{:S(2)}, u32[]{:S(2)}) collective-permute-start(bf16[800,128]{1,0:T(8,128)(2,1)} %param.3), channel_id=1, source_target_pairs={{1,0},{2,1},{3,2},{4,3},{5,4},{6,5},{7,6},{8,7},{9,8},{10,9},{11,1... | collective-permute-start | bytes 614408 | tf_op jit(solution)/shard_map/ppermute | solution.py:20
  18.8 18.8 %collective-permute-start = (bf16[800,128]{1,0:T(8,128)(2,1)}, bf16[800,128]{1,0:T(8,128)(2,1)S(1)}, u32[]{:S(2)}, u32[]{:S(2)}) collective-permute-start(bf16[800,128]{1,0:T(8,128)(2,1)} %param.3), channel_id=1, source_target_pairs={{0,1},{1,2},{2,3},{3,4},{4,5},{5,6},{6,7},{7,8},{8,9},{9,10},{10,1... | collective-permute-start | bytes 614408 | tf_op jit(solution)/shard_map/ppermute | solution.py:18
  39.7 145.8 %all-gather.6.cloned.1.call-start = ((), (), s32[]{:S(2)}) async-start(), calls=%async_computation.2 | async-start | bytes 8192000 | tf_op jit(solution)/shard_map/all_gather | solution.py:36
  111.8 112.6 %all-gather.8.cloned.1.call-start = ((), (), s32[]{:S(2)}) async-start(), calls=%async_computation.3 | async-start | bytes 19660800 | tf_op jit(solution)/shard_map/all_gather | solution.py:36
  224.4 6.6 %copy-start.1 = (bf16[800,2,128]{2,0,1:T(8,128)(2,1)S(1)}, bf16[800,2,128]{2,0,1:T(8,128)(2,1)}, u32[]{:S(2)}) copy-start(bf16[800,2,128]{2,0,1:T(8,128)(2,1)} %convolution_convert_fusion) | copy-start | bytes 1228804
Sparse Core Ops, SparseCore 0:
  39.8 71.9 all-gather.3
  113.9 71.5 all-gather.5
  187.6 36.7 all-gather.7
where the time goes:
time: 298 us; the launch traced here: 297 us
  waiting for transfers between devices  201 us (67%)
  blocking collectives  56.7 us (19%)
  starting transfers between devices  14.3 us (5%)
  between operations  13.2 us (4%)
  local copies, waits for them, and re-layouts  6.8 us (2%)
  matrix products  5.05 us (2%)
    all_gather x3, waiting for transfers between devices, gather_in_order(): blocks = lax.all_gather(blocks, axes[k], axis=0, tiled=True)  184 us
    all_to_all x1, blocking collectives, sum_at_owner(): lax.all_to_all(blocks, axis, split_axis=0, concat_axis=0, tiled=True)  56.7 us
    ppermute x1, starting transfers between devices, padded_2(): lax.ppermute(head, axis, [((i + 1) % count, i) for i in range(ends)])  12.3 us
    ppermute x1, waiting for transfers between devices, padded_2(): lax.ppermute(tail, axis, [(i, (i + 1) % count) for i in range(ends)])  8.6 us
    ppermute x1, waiting for transfers between devices, padded_2(): lax.ppermute(head, axis, [((i + 1) % count, i) for i in range(ends)])  8.28 us
    transpose x1, local copies, waits for them, and re-layouts, gather_in_order(): blocks.transpose(*turned, *range(len(turns), blocks.ndim))  6.59 us
  transfers between devices with their start and end apart: 5, of which 5 were waited for; matrix products, arithmetic and copies ran while one was open for 0% of the time, Pallas kernels for 0%

commit v1 on v0

--- a/solution.py
+++ b/solution.py
@@ -33,7 +33,8 @@
 def gather_in_order(shard, axes, turns):
     blocks = shard[None]
     for k in turns:
-        blocks = lax.all_gather(blocks, axes[k], axis=0, tiled=True)
+        sent = jnp.stack([blocks] * lax.axis_size(axes[k]))
+        blocks = jnp.concatenate(lax.all_to_all(sent, axes[k], 0, 0), axis=0)
     held = [lax.axis_size(axes[k]) for k in reversed(turns)]
     blocks = blocks.reshape(*held, *shard.shape)
     turned = sorted(range(len(turns)), key=lambda place: turns[len(turns) - 1 - place])

time: 298 us -> 274 us (0.919)
  the two profiles are of different devices: /device:TPU:2 before, /device:TPU:32 now
where the time goes in v1:
time: 274 us; the launch traced here: 273 us
  blocking collectives  173 us (63%)
  waiting for transfers between devices  67.8 us (25%)
  starting transfers between devices  14.8 us (5%)
  other arithmetic  7.26 us (3%)
  local copies, waits for them, and re-layouts  6.1 us (2%)
  matrix products  4.29 us (2%)
    all_to_all x2, blocking collectives, gather_in_order(): blocks = jnp.concatenate(lax.all_to_all(sent, axes[k], 0, 0), axis=0)  113 us
    all_to_all x1, waiting for transfers between devices, gather_in_order(): blocks = jnp.concatenate(lax.all_to_all(sent, axes[k], 0, 0), axis=0)  66.5 us
    all_to_all x1, blocking collectives, sum_at_owner(): lax.all_to_all(blocks, axis, split_axis=0, concat_axis=0, tiled=True)  60.1 us
    all_to_all x1, starting transfers between devices, gather_in_order(): blocks = jnp.concatenate(lax.all_to_all(sent, axes[k], 0, 0), axis=0)  10.4 us
    another operation x1, other arithmetic, gather_in_order(): sent = jnp.stack([blocks] * lax.axis_size(axes[k]))  6.47 us
  transfers between devices with their start and end apart: 3, of which 2 were waited for; matrix products, arithmetic and copies ran while one was open for 0% of the time, Pallas kernels for 0%

profile of v1, /device:TPU:32, one launch (start us, length us, event | category | flops | bytes accessed | tf_op | source)
XLA Modules:
  0.0 273.4 jit_solution(1958488849572521753)
XLA Ops:
  0.0 0.0 copy-start
  0.0 1.4 collective-permute-start.1
  1.4 3.0 %collective-permute-start = (bf16[800,128]{1,0:T(8,128)(2,1)}, bf16[800,128]{1,0:T(8,128)(2,1)S(1)}, u32[]{:S(2)}, u32[]{:S(2)}) collective-permute-start(bf16[800,128]{1,0:T(8,128)(2,1)} %param.3), channel_id=1, source_target_pairs={{0,1},{1,2},{2,3},{3,4},{4,5},{5,6},{6,7},{7,8},{8,9},{9,10},{10,1... | collective-permute-start | bytes 614408 | tf_op jit(solution)/shard_map/ppermute | solution.py:18
  4.5 0.0 collective-permute-done.1
  4.5 1.3 collective-permute-done
  5.7 0.0 copy-done
  5.7 1.3 convolution_convert_fusion
  7.0 0.2 stack.9
  7.3 90.7 %all_to_all.20 = bf16[4,1,1600,128]{3,2,1,0:T(8,128)(2,1)S(1)} all-to-all(bf16[4,1,1600,128]{3,2,1,0:T(8,128)(2,1)S(1)} %stack.9), channel_id=1, replica_groups=mesh['aux'=16,'row_0'=4,'row_1'=4,'row_2'=2] {'row_1'}, dimensions={0} | all-to-all | bytes 3276800 | tf_op jit(solution)/shard_map/all_to_all | solution.py:37
  98.0 4.0 %stack.10 = bf16[4,4,1600,128]{3,2,1,0:T(8,128)(2,1)} broadcast(bf16[4,1600,128]{2,1,0:T(8,128)(2,1)S(1)} %bitcast.37), dimensions={1,2,3} | broadcast | bytes 8192000 | tf_op jit(solution)/shard_map/stack | solution.py:36
  101.9 10.4 %all-to-all-start.1 = ((bf16[4,4,1600,128]{3,2,1,0:T(8,128)(2,1)}), bf16[4,4,1600,128]{3,2,1,0:T(8,128)(2,1)}, u32[]{:S(2)}, u32[]{:S(2)}) async-start(bf16[4,4,1600,128]{3,2,1,0:T(8,128)(2,1)} %stack.10), calls=%async_computation.1 | async-start | bytes 13107200 | tf_op jit(solution)/shard_map/all_to_all | solution.py:37
  112.3 0.9 fusion.10
  113.2 66.5 %all-to-all-done.1 = bf16[4,4,1600,128]{3,2,1,0:T(8,128)(2,1)} async-done(((bf16[4,4,1600,128]{3,2,1,0:T(8,128)(2,1)}), bf16[4,4,1600,128]{3,2,1,0:T(8,128)(2,1)}, u32[]{:S(2)}, u32[]{:S(2)}) %all-to-all-start.1) | async-done | bytes 6553632 | tf_op jit(solution)/shard_map/all_to_all | solution.py:37
  179.8 6.5 %pad_maximum_fusion = bf16[2,16,1600,128]{3,2,1,0:T(8,128)(2,1)S(1)} fusion(bf16[1,16,1600,128]{3,2,1,0:T(8,128)(2,1)} %bitcast.5), kind=kLoop, calls=%fused_computation.3 | loop fusion | flops 6553600 | bytes 19660800 | tf_op jit(solution)/shard_map/stack | solution.py:36
  186.2 22.3 %all_to_all.21 = bf16[2,16,1600,128]{3,2,1,0:T(8,128)(2,1)S(1)} all-to-all(bf16[2,16,1600,128]{3,2,1,0:T(8,128)(2,1)S(1)} %pad_maximum_fusion), channel_id=1, replica_groups=mesh['aux'=16,'row_0'=4,'row_1'=4,'row_2'=2] {'row_2'}, dimensions={0} | all-to-all | bytes 26214400 | tf_op jit(solution)/shard_map/all_to_all | solution.py:37
  208.5 1.7 copy.8
  210.2 2.1 fusion.3
  212.4 0.2 copy.20
  212.6 60.1 %all_to_all.22 = f32[16,128,256]{2,1,0:T(8,128)S(1)} all-to-all(f32[16,128,256]{2,1,0:T(8,128)S(1)} %bitcast.36), channel_id=1, replica_groups=mesh['aux'=16,'row_0'=4,'row_1'=4,'row_2'=2] {'aux'}, dimensions={0} | all-to-all | bytes 4194304 | tf_op jit(solution)/shard_map/all_to_all | solution.py:55
  272.7 0.8 reduce_sum.9
  (1 shorter events, 0.0 us)
Async XLA Ops:
  0.0 5.7 %copy-start = (bf16[2,384,128]{2,1,0:T(8,128)(2,1)S(1)}, bf16[2,384,128]{2,1,0:T(8,128)(2,1)}, u32[]{:S(2)}) copy-start(bf16[2,384,128]{2,1,0:T(8,128)(2,1)} %param.4) | copy-start | bytes 589828
  0.0 4.5 %collective-permute-start.1 = (bf16[800,128]{1,0:T(8,128)(2,1)}, bf16[800,128]{1,0:T(8,128)(2,1)S(1)}, u32[]{:S(2)}, u32[]{:S(2)}) collective-permute-start(bf16[800,128]{1,0:T(8,128)(2,1)} %param.3), channel_id=1, source_target_pairs={{1,0},{2,1},{3,2},{4,3},{5,4},{6,5},{7,6},{8,7},{9,8},{10,9},{11,1... | collective-permute-start | bytes 614408 | tf_op jit(solution)/shard_map/ppermute | solution.py:20
  1.4 4.3 %collective-permute-start = (bf16[800,128]{1,0:T(8,128)(2,1)}, bf16[800,128]{1,0:T(8,128)(2,1)S(1)}, u32[]{:S(2)}, u32[]{:S(2)}) collective-permute-start(bf16[800,128]{1,0:T(8,128)(2,1)} %param.3), channel_id=1, source_target_pairs={{0,1},{1,2},{2,3},{3,4},{4,5},{5,6},{6,7},{7,8},{8,9},{9,10},{10,1... | collective-permute-start | bytes 614408 | tf_op jit(solution)/shard_map/ppermute | solution.py:18
  101.9 77.8 %all-to-all-start.1 = ((bf16[4,4,1600,128]{3,2,1,0:T(8,128)(2,1)}), bf16[4,4,1600,128]{3,2,1,0:T(8,128)(2,1)}, u32[]{:S(2)}, u32[]{:S(2)}) async-start(bf16[4,4,1600,128]{3,2,1,0:T(8,128)(2,1)} %stack.10), calls=%async_computation.1 | async-start | bytes 13107200 | tf_op jit(solution)/shard_map/all_to_all | solution.py:37
